TPU v7x, 32 devices: a whole 2x2x4 slice. The times are simulated.
32 devices in a mesh: dp: 16 (over z, x, core), tensor: 2 (over y).
Axes of the slice: x: 2, y: 2, z: 4, core: 2. Of those that a mesh axis runs over, the one named last changes fastest.
Arguments:
- tokens: bfloat16 [8192, 1152], P(('dp', 'tensor')), may hold values from -6 to 6
- condition: bfloat16 [32, 1152], P(('dp', 'tensor')), may hold values from -6 to 6
- w_qkv: bfloat16 [1152, 3, 1152], P('dp', None, 'tensor'), may hold values from -0.1875 to 0.1875
- qv_bias: bfloat16 [2, 1152], P(None, 'tensor'), may hold values from -3 to 3
- w_proj: bfloat16 [1152, 1152], P('tensor', 'dp'), may hold values from -1 to 1
- proj_bias: bfloat16 [1152], replicated, may hold values from -3 to 3
- w_fc1: bfloat16 [1152, 4608], P('dp', 'tensor'), may hold values from -0.1875 to 0.1875
- fc1_bias: bfloat16 [4608], P('tensor'), may hold values from -3 to 3
- w_fc2: bfloat16 [4608, 1152], P('tensor', 'dp'), may hold values from -0.09375 to 0.09375
- fc2_bias: bfloat16 [1152], replicated, may hold values from -3 to 3
- w_ada: bfloat16 [1152, 6912], P(None, ('dp', 'tensor')), may hold values from -0.1875 to 0.1875
- ada_bias: bfloat16 [6912], P(('dp', 'tensor')), may hold values from -3 to 3
- cotangent: bfloat16 [8192, 1152], P(('dp', 'tensor')), may hold values from -6 to 6
Outputs:
- output: bfloat16 [8192, 1152], P(('dp', 'tensor'))
- grad_tokens: float32 [8192, 1152], P(('dp', 'tensor'))
- grad_condition: float32 [32, 1152], P(('dp', 'tensor'))
- grad_w_qkv: float32 [1152, 3, 1152], P('dp', None, 'tensor')
- grad_qv_bias: float32 [2, 1152], P(None, 'tensor')
- grad_w_proj: float32 [1152, 1152], P('tensor', 'dp')
- grad_proj_bias: float32 [1152], replicated
- grad_w_fc1: float32 [1152, 4608], P('dp', 'tensor')
- grad_fc1_bias: float32 [4608], P('tensor')
- grad_w_fc2: float32 [4608, 1152], P('tensor', 'dp')
- grad_fc2_bias: float32 [1152], replicated
- grad_w_ada: float32 [1152, 6912], P(None, ('dp', 'tensor'))
- grad_ada_bias: float32 [6912], P(('dp', 'tensor'))
All inputs are finite; a program needn't handle non-finite values.
Results may differ from a plain program's by a relative error of at most 0.015.
The roundings to bfloat16 on the way count: a program that leaves them out, or rounds other values in their place, can miss the bound.
Values may be sent and summed in bfloat16 or wider, within the bound.
A program may use at most 128 MiB of HBM per device.

v0:
```python
from functools import partial
import math
import jax
import jax.numpy as jnp
from jax import lax
from jax.sharding import PartitionSpec as P

HEAD_DIM = 72
eps = 1e-06


def normalize(values):
    center = values - jnp.mean(values, axis=-1, keepdims=True)
    spread = lax.rsqrt(jnp.mean(center * center, axis=-1, keepdims=True) + eps)
    return (center * spread, spread)


def norm_back(gradient, normed, spread):
    return spread * (
        gradient
        - jnp.mean(gradient, axis=-1, keepdims=True)
        - normed * jnp.mean(gradient * normed, axis=-1, keepdims=True)
    )


def contract_last(left_side, right_side):
    return lax.dot_general(
        left_side, right_side, (((1,), (1,)), ((), ())), preferred_element_type=jnp.float32
    )


def contract_first(left_side, right_side):
    return lax.dot_general(
        left_side, right_side, (((0,), (0,)), ((), ())), preferred_element_type=jnp.float32
    )


def gather_rows(values):
    return lax.all_gather(values, "tensor", axis=0, tiled=True)


def gather_grads(values):
    return lax.all_gather(values, "tensor", axis=0, tiled=True)


def sum_rows(source, weight, own_rows):

    def row_term(first_row, number):
        return jnp.dot(source, weight, preferred_element_type=jnp.float32)

    return lax.psum_scatter(
        row_term(jnp.int32(0), lax.axis_size("tensor") * own_rows).astype(jnp.bfloat16),
        "tensor",
        scatter_dimension=0,
        tiled=True,
    ).astype(jnp.float32)


def sum_grads(source, weight, own_rows):

    def row_term(first_row, number):
        return contract_last(source, weight)

    return lax.psum_scatter(
        row_term(jnp.int32(0), lax.axis_size("tensor") * own_rows).astype(jnp.bfloat16),
        "tensor",
        scatter_dimension=0,
        tiled=True,
    ).astype(jnp.float32)


def attend(block):
    query_rows, key_rows, value_rows = block
    scaling = query_rows.shape[-1] ** (-0.5)
    scores = (
        jnp.einsum("sqhe,skhe->shqk", query_rows, key_rows, preferred_element_type=jnp.float32)
        * scaling
    )
    highest = jnp.max(scores, axis=-1, keepdims=True)
    expons = jnp.exp(scores - highest)
    summed = jnp.sum(expons, axis=-1, keepdims=True)
    probs = (expons / summed).astype(jnp.bfloat16)
    mixed = jnp.einsum("shqk,skhe->sqhe", probs, value_rows, preferred_element_type=jnp.float32)
    return (mixed.astype(jnp.bfloat16), (highest + jnp.log(summed))[..., 0])


def attend_back(block):
    query_rows, key_rows, value_rows, logsum, grad_mixed = block
    scaling = query_rows.shape[-1] ** (-0.5)
    scores = (
        jnp.einsum("sqhe,skhe->shqk", query_rows, key_rows, preferred_element_type=jnp.float32)
        * scaling
    )
    probs = jnp.exp(scores - logsum[..., None])
    grad_probs = jnp.einsum(
        "sqhe,skhe->shqk", grad_mixed, value_rows, preferred_element_type=jnp.float32
    )
    grad_values = jnp.einsum(
        "shqk,sqhe->skhe",
        probs.astype(jnp.bfloat16),
        grad_mixed,
        preferred_element_type=jnp.float32,
    )
    grad_scores = (
        probs * (grad_probs - jnp.sum(grad_probs * probs, axis=-1, keepdims=True))
    ).astype(jnp.bfloat16)
    grad_queries = (
        jnp.einsum("shqk,skhe->sqhe", grad_scores, key_rows, preferred_element_type=jnp.float32)
        * scaling
    )
    grad_keys = (
        jnp.einsum("shqk,sqhe->skhe", grad_scores, query_rows, preferred_element_type=jnp.float32)
        * scaling
    )
    return (
        grad_queries.astype(jnp.bfloat16),
        grad_keys.astype(jnp.bfloat16),
        grad_values.astype(jnp.bfloat16),
    )


def per_device(
    tokens,
    condition,
    w_qkv,
    qv_bias,
    w_proj,
    proj_bias,
    w_fc1,
    fc1_bias,
    w_fc2,
    fc2_bias,
    w_ada,
    ada_bias,
    cotangent,
):
    own_rows, width = tokens.shape
    own_seqs = condition.shape[0]
    length = own_rows // own_seqs
    group_rows = own_rows * lax.axis_size("tensor")
    group_seqs = group_rows // length
    local_width = w_qkv.shape[2]
    local_heads = local_width // HEAD_DIM
    block_seqs = math.gcd(group_seqs, max(1, 512 // length))
    blocks = group_seqs // block_seqs
    head_shape = (blocks, block_seqs, length, local_heads, HEAD_DIM)
    cond_float = condition.astype(jnp.float32)
    silu_cond = jax.nn.silu(cond_float).astype(jnp.bfloat16)
    every_cond = lax.all_gather(silu_cond, ("dp", "tensor"), axis=0, tiled=True)
    columns = (
        jnp.dot(every_cond, w_ada, preferred_element_type=jnp.float32)
        + ada_bias.astype(jnp.float32)
    ).astype(jnp.bfloat16)
    modulation = lax.all_to_all(columns, ("dp", "tensor"), split_axis=0, concat_axis=1, tiled=True)
    modul = modulation.astype(jnp.float32).reshape(own_seqs, 6, 1, width)
    shift_attn = modul[:, 0]
    scale_attn = modul[:, 1]
    gate_attn = modul[:, 2]
    shift_mlp = modul[:, 3]
    scale_mlp = modul[:, 4]
    gate_mlp = modul[:, 5]
    qkv_full, proj_full, fc1_full, fc2_full = (
        lax.all_gather(w_qkv, "dp", axis=0, tiled=True),
        lax.all_gather(w_proj, "dp", axis=1, tiled=True),
        lax.all_gather(w_fc1, "dp", axis=0, tiled=True),
        lax.all_gather(w_fc2, "dp", axis=1, tiled=True),
    )
    residual = tokens.astype(jnp.float32).reshape(own_seqs, length, width)
    normed_attn, spread_attn = normalize(residual)
    attn_input = (
        (normed_attn * (1.0 + scale_attn) + shift_attn)
        .astype(jnp.bfloat16)
        .reshape(own_rows, width)
    )
    attn_rows = gather_rows(attn_input)
    projected = jnp.einsum("td,dkf->tkf", attn_rows, qkv_full, preferred_element_type=jnp.float32)
    bias_float = qv_bias.astype(jnp.float32)
    queries = (projected[:, 0] + bias_float[0]).astype(jnp.bfloat16).reshape(head_shape)
    key_all = projected[:, 1].astype(jnp.bfloat16).reshape(head_shape)
    value_all = (projected[:, 2] + bias_float[1]).astype(jnp.bfloat16).reshape(head_shape)
    mixed, logsum = lax.map(attend, (queries, key_all, value_all))
    mixed_rows = mixed.reshape(group_rows, local_width)
    attn_out = (sum_rows(mixed_rows, proj_full, own_rows) + proj_bias.astype(jnp.float32)).reshape(
        own_seqs, length, width
    )
    middle = residual + gate_attn * attn_out
    normed_mlp, spread_mlp = normalize(middle)
    mlp_input = (
        (normed_mlp * (1.0 + scale_mlp) + shift_mlp).astype(jnp.bfloat16).reshape(own_rows, width)
    )
    mlp_rows = gather_rows(mlp_input)
    upper = jnp.dot(mlp_rows, fc1_full, preferred_element_type=jnp.float32) + fc1_bias.astype(
        jnp.float32
    )
    hidden = jax.nn.gelu(upper, approximate=True).astype(jnp.bfloat16)
    mlp_out = (sum_rows(hidden, fc2_full, own_rows) + fc2_bias.astype(jnp.float32)).reshape(
        own_seqs, length, width
    )
    output = (middle + gate_mlp * mlp_out).astype(jnp.bfloat16).reshape(own_rows, width)
    qkv_back, proj_back, fc1_back, fc2_back = (
        lax.all_gather(w_qkv, "dp", axis=0, tiled=True),
        lax.all_gather(w_proj, "dp", axis=1, tiled=True),
        lax.all_gather(w_fc1, "dp", axis=0, tiled=True),
        lax.all_gather(w_fc2, "dp", axis=1, tiled=True),
    )
    grad_out = cotangent.astype(jnp.float32).reshape(own_seqs, length, width)
    grad_mlp = (gate_mlp * grad_out).astype(jnp.bfloat16).reshape(own_rows, width)
    grad_gate_mlp = jnp.sum(grad_out * mlp_out, axis=1)
    grad_mlp_rows = gather_grads(grad_mlp)
    fc2_bias_grad = jnp.sum(grad_mlp_rows.astype(jnp.float32), axis=0)
    fc2_grad = contract_first(hidden, grad_mlp_rows)
    grad_hidden = contract_last(grad_mlp_rows, fc2_back)
    ignored, gelu_pull = jax.vjp(partial(jax.nn.gelu, approximate=True), upper)
    grad_upper = gelu_pull(grad_hidden)[0].astype(jnp.bfloat16)
    fc1_bias_grad = jnp.sum(grad_upper.astype(jnp.float32), axis=0)
    fc1_grad = contract_first(mlp_rows, grad_upper)
    grad_mlp_input = sum_grads(grad_upper, fc1_back, own_rows).reshape(own_seqs, length, width)
    grad_shift_mlp = jnp.sum(grad_mlp_input, axis=1)
    grad_scale_mlp = jnp.sum(grad_mlp_input * normed_mlp, axis=1)
    grad_middle = grad_out + norm_back(grad_mlp_input * (1.0 + scale_mlp), normed_mlp, spread_mlp)
    grad_attn = (gate_attn * grad_middle).astype(jnp.bfloat16).reshape(own_rows, width)
    grad_gate_attn = jnp.sum(grad_middle * attn_out, axis=1)
    grad_attn_rows = gather_grads(grad_attn)
    proj_bias_grad = jnp.sum(grad_attn_rows.astype(jnp.float32), axis=0)
    proj_grad = contract_first(mixed_rows, grad_attn_rows)
    grad_mixed = contract_last(grad_attn_rows, proj_back).astype(jnp.bfloat16).reshape(head_shape)
    grad_query, grad_key, grad_value = lax.map(
        attend_back, (queries, key_all, value_all, logsum, grad_mixed)
    )
    grad_qkv = jnp.stack(
        [
            grad_query.reshape(group_rows, local_width),
            grad_key.reshape(group_rows, local_width),
            grad_value.reshape(group_rows, local_width),
        ],
        axis=1,
    )
    qv_bias_grad = jnp.stack(
        [
            jnp.sum(grad_qkv[:, 0].astype(jnp.float32), axis=0),
            jnp.sum(grad_qkv[:, 2].astype(jnp.float32), axis=0),
        ],
        axis=0,
    )
    qkv_grad = jnp.einsum("td,tkf->dkf", attn_rows, grad_qkv, preferred_element_type=jnp.float32)
    grad_attn_input = sum_grads(
        grad_qkv.reshape(group_rows, 3 * local_width),
        qkv_back.reshape(width, 3 * local_width),
        own_rows,
    ).reshape(own_seqs, length, width)
    grad_shift_attn = jnp.sum(grad_attn_input, axis=1)
    grad_scale_attn = jnp.sum(grad_attn_input * normed_attn, axis=1)
    grad_tokens = (
        grad_middle + norm_back(grad_attn_input * (1.0 + scale_attn), normed_attn, spread_attn)
    ).reshape(own_rows, width)
    grad_modulation = (
        jnp.stack(
            [
                grad_shift_attn,
                grad_scale_attn,
                grad_gate_attn,
                grad_shift_mlp,
                grad_scale_mlp,
                grad_gate_mlp,
            ],
            axis=1,
        )
        .reshape(own_seqs, 6 * width)
        .astype(jnp.bfloat16)
    )
    qkv_grad, proj_grad, fc1_grad, fc2_grad = (
        lax.psum_scatter(qkv_grad, "dp", scatter_dimension=0, tiled=True),
        lax.psum_scatter(proj_grad, "dp", scatter_dimension=1, tiled=True),
        lax.psum_scatter(fc1_grad, "dp", scatter_dimension=0, tiled=True),
        lax.psum_scatter(fc2_grad, "dp", scatter_dimension=1, tiled=True),
    )
    qv_bias_grad, proj_bias_grad, fc1_bias_grad, fc2_bias_grad = lax.psum(
        (qv_bias_grad, proj_bias_grad, fc1_bias_grad, fc2_bias_grad), "dp"
    )
    grad_columns = lax.all_to_all(
        grad_modulation, ("dp", "tensor"), split_axis=1, concat_axis=0, tiled=True
    )
    ada_grad = contract_first(every_cond, grad_columns)
    ada_bias_grad = jnp.sum(grad_columns.astype(jnp.float32), axis=0)
    grad_silu = lax.psum_scatter(
        contract_last(grad_columns, w_ada), ("dp", "tensor"), scatter_dimension=0, tiled=True
    )
    ignored_cond, silu_pull = jax.vjp(jax.nn.silu, cond_float)
    grad_condition = silu_pull(grad_silu)[0]
    return (
        output,
        grad_tokens,
        grad_condition,
        qkv_grad,
        qv_bias_grad,
        proj_grad,
        proj_bias_grad,
        fc1_grad,
        fc1_bias_grad,
        fc2_grad,
        fc2_bias_grad,
        ada_grad,
        ada_bias_grad,
    )


def solution(mesh):
    placed = (
        P(("dp", "tensor"), None),
        P(("dp", "tensor"), None),
        P("dp", None, "tensor"),
        P(None, "tensor"),
        P("tensor", "dp"),
        P(),
        P("dp", "tensor"),
        P("tensor"),
        P("tensor", "dp"),
        P(),
        P(None, ("dp", "tensor")),
        P(("dp", "tensor")),
        P(("dp", "tensor"), None),
    )
    return jax.shard_map(
        per_device,
        mesh=mesh,
        in_specs=placed,
        out_specs=(
            P(("dp", "tensor"), None),
            P(("dp", "tensor"), None),
            P(("dp", "tensor"), None),
            P("dp", None, "tensor"),
            P(None, "tensor"),
            P("tensor", "dp"),
            P(),
            P("dp", "tensor"),
            P("tensor"),
            P("tensor", "dp"),
            P(),
            P(None, ("dp", "tensor")),
            P(("dp", "tensor")),
        ),
        check_vma=False,
    )
```

profile of v0, /device:TPU:0, one launch (start us, length us, event | category | flops | bytes accessed | tf_op | source)
XLA Modules:
  0.0 1101.5 jit_solution(12984828745104131564)
XLA Ops:
  8.0 70.5 %all-gather = bf16[32,1,1152]{2,1,0:T(2,128)(2,1)S(1)} all-gather(bf16[1,1,1152]{2,1,0:T(2,128)(2,1)S(1)} %get-tuple-element.80), channel_id=1, replica_groups=mesh['dp'=16,'tensor'=2] {'dp','tensor'}, dimensions={0}, use_global_device_ids=true | all-gather | bytes 76032 | tf_op jit(solution)/shard_map/all_gather | solution.py:149
  80.1 2.6 all-to-all-start
  83.2 6.8 all-to-all-done
  93.2 17.5 %all-gather.10.cloned.1.call-done = bf16[512,1152]{1,0:T(8,128)(2,1)} async-done(((bf16[256,1152]{1,0:T(8,128)(2,1)}), bf16[512,1152]{1,0:T(8,128)(2,1)}) %all-gather.10.cloned.1.call-update) | async-done | bytes 1179664 | tf_op jit(solution)/shard_map/all_gather | solution.py:39
  110.7 53.9 %all-gather.12.cloned.1.call-done = bf16[1152,3,576]{2,0,1:T(8,128)(2,1)} async-done(((bf16[72,3,576]{2,0,1:T(8,128)(2,1)}), bf16[1152,3,576]{2,0,1:T(8,128)(2,1)}) %all-gather.12.cloned.1.call-update) | async-done | bytes 3981328 | tf_op jit(solution)/shard_map/all_gather | solution.py:163
  164.6 5.2 fusion.53
  172.6 1.9 convert_element_type.196
  174.6 2.9 squeeze.35
  182.3 22.1 %all-gather.14.cloned.1.call-done = bf16[576,1152]{0,1:T(8,128)(2,1)} async-done(((bf16[576,72]{0,1:T(8,128)(2,1)}), bf16[576,1152]{0,1:T(8,128)(2,1)}) %all-gather.14.cloned.1.call-update) | async-done | bytes 1327120 | tf_op jit(solution)/shard_map/all_gather | solution.py:164
  204.4 3.6 convolution_convert_fusion.2
  211.8 17.1 %reduce-scatter.11.cloned.1.call-done = bf16[256,1152]{1,0:T(8,128)(2,1)} async-done(((bf16[512,1152]{1,0:T(8,128)(2,1)}), bf16[256,1152]{1,0:T(8,128)(2,1)}) %reduce-scatter.11.cloned.1.call-update) | async-done | bytes 589840 | tf_op jit(solution)/shard_map/reduce_scatter | solution.py:51
  228.9 1.4 fusion.85
  233.9 19.7 %all-gather.22.cloned.1.call-done = bf16[512,1152]{1,0:T(8,128)(2,1)} async-done(((bf16[256,1152]{1,0:T(8,128)(2,1)}), bf16[512,1152]{1,0:T(8,128)(2,1)}) %all-gather.22.cloned.1.call-update) | async-done | bytes 1179664 | tf_op jit(solution)/shard_map/all_gather | solution.py:43
  253.6 58.4 %all-gather.20.cloned.1.call-done = bf16[2304,1152]{0,1:T(8,128)(2,1)} async-done(((bf16[2304,72]{0,1:T(8,128)(2,1)}), bf16[2304,1152]{0,1:T(8,128)(2,1)}) %all-gather.20.cloned.1.call-update) | async-done | bytes 5308432 | tf_op jit(solution)/shard_map/all_gather | solution.py:166
  312.0 8.2 fusion.89
  320.2 48.9 %all-gather.18.cloned.1.call-done = bf16[1152,2304]{1,0:T(8,128)(2,1)} async-done(((bf16[72,2304]{1,0:T(8,128)(2,1)}), bf16[1152,2304]{1,0:T(8,128)(2,1)}) %all-gather.18.cloned.1.call-update) | async-done | bytes 5308432 | tf_op jit(solution)/shard_map/all_gather | solution.py:165
  369.1 23.5 %all-gather.16.cloned.1.call-done = bf16[512,1152]{1,0:T(8,128)(2,1)} async-done(((bf16[256,1152]{1,0:T(8,128)(2,1)}), bf16[512,1152]{1,0:T(8,128)(2,1)}) %all-gather.16.cloned.1.call-update) | async-done | bytes 1179664 | tf_op jit(solution)/shard_map/all_gather | solution.py:39
  392.6 10.6 convert_reduce_fusion
  404.6 4.2 convolution_convert_fusion
  408.9 9.1 convolution_convert_fusion.1
  418.7 12.1 %reduce-scatter.15.cloned.1.call-done = bf16[256,1152]{1,0:T(8,128)(2,1)} async-done(((bf16[512,1152]{1,0:T(8,128)(2,1)}), bf16[256,1152]{1,0:T(8,128)(2,1)}) %reduce-scatter.15.cloned.1.call-update) | async-done | bytes 589840 | tf_op jit(solution)/shard_map/reduce_scatter | solution.py:64
  430.8 2.4 fusion.46
  433.8 21.0 %reduce-scatter.13.cloned.1.call-done = bf16[256,1152]{1,0:T(8,128)(2,1)} async-done(((bf16[512,1152]{1,0:T(8,128)(2,1)}), bf16[256,1152]{1,0:T(8,128)(2,1)}) %reduce-scatter.13.cloned.1.call-update) | async-done | bytes 589840 | tf_op jit(solution)/shard_map/reduce_scatter | solution.py:51
  454.8 4.0 multiply_reduce_fusion.2
  461.0 22.7 %all-gather.24.cloned.1.call-done = bf16[512,1152]{1,0:T(8,128)(2,1)} async-done(((bf16[256,1152]{1,0:T(8,128)(2,1)}), bf16[512,1152]{1,0:T(8,128)(2,1)}) %all-gather.24.cloned.1.call-update) | async-done | bytes 1179664 | tf_op jit(solution)/shard_map/all_gather | solution.py:43
  483.7 3.5 convolution_convert_fusion.3
  487.2 1.9 squeeze.37
  489.1 3.4 convert_reduce_fusion.4
  492.9 1.6 multiply_reduce_fusion
  496.2 1.6 fusion.31
  498.8 1.7 copy.79
  503.2 6.2 fusion.8
  510.7 20.8 %reduce-scatter.17.cloned.1.call-done = bf16[256,1152]{1,0:T(8,128)(2,1)} async-done(((bf16[512,1152]{1,0:T(8,128)(2,1)}), bf16[256,1152]{1,0:T(8,128)(2,1)}) %reduce-scatter.17.cloned.1.call-update) | async-done | bytes 589840 | tf_op jit(solution)/shard_map/reduce_scatter | solution.py:64
  531.5 2.4 fusion.48
  534.2 11.8 %all_to_all.26 = bf16[1,32,216]{2,0,1:T(2,128)(2,1)S(1)} all-to-all(bf16[1,32,216]{2,0,1:T(2,128)(2,1)S(1)} %convert_element_type.235), channel_id=1, replica_groups=mesh['dp'=16,'tensor'=2] {'dp','tensor'}, dimensions={1} | all-to-all | bytes 27648 | tf_op jit(solution)/shard_map/all_to_all | solution.py:280
  546.9 2.8 fusion.90
  551.2 7.3 fusion.51
  559.8 8.7 fusion.91
  569.8 9.3 fusion.86
  579.2 1.6 convert_reduce_fusion.1
  580.9 1.5 convert_reduce_fusion.2
  582.4 58.3 %all-reduce.2 = (f32[2,576]{1,0:T(2,128)}, f32[1152]{0:T(1024)}, f32[2304]{0:T(1024)}, f32[1152]{0:T(1024)}) all-reduce(f32[2,576]{1,0:T(2,128)S(1)} %pad_maximum_fusion, f32[1152]{0:T(1024)S(1)} %convert_reduce_fusion.2, f32[2304]{0:T(1024)S(1)} %copy-done.28, ...), channel_id=1, replica_groups=mesh['dp'=16,'tensor'=2] {'dp'}, use_global_device_ids=true, to_apply=%region_25.26 | all-reduce | flops 5760 | bytes 46080 | tf_op jit(solution)/shard_map/psum | solution.py:277
  640.8 1.5 fusion.41
  644.2 21.4 %all-reduce.5.cloned.1.call-done = f32[32,1152]{1,0:T(8,128)} async-done(((f32[32,1152]{1,0:T(8,128)}), f32[32,1152]{1,0:T(8,128)}) %all-reduce.5.cloned.1.call-update) | async-done | bytes 147472
  667.0 69.2 %reduce-scatter.25.cloned.1.call-done = f32[576,72]{0,1:T(8,128)} async-done(((f32[576,1152]{0,1:T(8,128)}), f32[576,72]{0,1:T(8,128)}) %reduce-scatter.25.cloned.1.call-update) | async-done | bytes 165904
  736.1 109.2 %reduce-scatter.19.cloned.1.call-done = f32[72,3,576]{2,0,1:T(8,128)} async-done(((f32[1152,3,576]{2,0,1:T(8,128)}), f32[72,3,576]{2,0,1:T(8,128)}) %reduce-scatter.19.cloned.1.call-update) | async-done | bytes 497680 | tf_op jit(solution)/shard_map/reduce_scatter | solution.py:272
  845.3 124.5 %reduce-scatter.21.cloned.1.call-done = f32[72,2304]{1,0:T(8,128)} async-done(((f32[1152,2304]{1,0:T(8,128)}), f32[72,2304]{1,0:T(8,128)}) %reduce-scatter.21.cloned.1.call-update) | async-done | bytes 663568 | tf_op jit(solution)/shard_map/reduce_scatter | solution.py:274
  969.8 124.8 %reduce-scatter.23.cloned.1.call-done = f32[2304,72]{0,1:T(8,128)} async-done(((f32[2304,1152]{0,1:T(8,128)}), f32[2304,72]{0,1:T(8,128)}) %reduce-scatter.23.cloned.1.call-update) | async-done | bytes 663568 | tf_op jit(solution)/shard_map/reduce_scatter | solution.py:275
  (170 shorter events, 41.4 us)
Async XLA Ops:
  7.2 71.9 %copy-start = (bf16[1152,216]{0,1:T(8,128)(2,1)S(1)}, bf16[1152,216]{0,1:T(8,128)(2,1)}, u32[]{:S(2)}) copy-start(bf16[1152,216]{0,1:T(8,128)(2,1)} %param.23) | copy-start | bytes 1492996
  7.2 75.5 %copy-start.3 = (bf16[256,1152]{1,0:T(8,128)(2,1)S(1)}, bf16[256,1152]{1,0:T(8,128)(2,1)}, u32[]{:S(2)}) copy-start(bf16[256,1152]{1,0:T(8,128)(2,1)} %param.13) | copy-start | bytes 1769476
  80.1 9.9 all-to-all-start
  82.6 28.0 %all-gather.10.cloned.1.call-start = ((), (), s32[]{:S(2)}) async-start(), calls=%async_computation.10 | async-start | bytes 1769472 | tf_op jit(solution)/shard_map/all_gather | solution.py:39
  83.2 9.7 copy-start.25
  83.2 9.8 copy-start.32
  91.4 73.2 %all-gather.12.cloned.1.call-start = ((), (), s32[]{:S(2)}) async-start(), calls=%async_computation.11 | async-start | bytes 4700160 | tf_op jit(solution)/shard_map/all_gather | solution.py:163
  92.2 112.2 %all-gather.14.cloned.1.call-start = ((), (), s32[]{:S(2)}) async-start(), calls=%async_computation.12 | async-start | bytes 1566720 | tf_op jit(solution)/shard_map/all_gather | solution.py:164
  92.9 136.0 %reduce-scatter.11.cloned.1.call-start = ((), (), s32[]{:S(2)}) async-start(), calls=%async_computation.13 | async-start | bytes 1769472 | tf_op jit(solution)/shard_map/reduce_scatter | solution.py:51
  178.4 2.0 copy-start.1
  178.4 2.1 copy-start.10
  182.3 25.7 %copy-start.12 = (bf16[72,8,2,256]{3,1,2,0:T(8,128)(2,1)}, bf16[72,8,2,256]{3,1,2,0:T(8,128)(2,1)S(1)}, u32[]{:S(2)}) copy-start(bf16[72,8,2,256]{3,1,2,0:T(8,128)(2,1)S(1)} %copy.93) | copy-start | bytes 1769476
  208.0 1.1 copy-start.14
  208.1 45.6 %all-gather.22.cloned.1.call-start = ((), (), s32[]{:S(2)}) async-start(), calls=%async_computation.18 | async-start | bytes 1769472 | tf_op jit(solution)/shard_map/all_gather | solution.py:43
  209.1 2.7 copy-start.31
  210.0 101.9 %all-gather.20.cloned.1.call-start = ((), (), s32[]{:S(2)}) async-start(), calls=%async_computation.16 | async-start | bytes 5640192 | tf_op jit(solution)/shard_map/all_gather | solution.py:166
  210.6 158.5 %all-gather.18.cloned.1.call-start = ((), (), s32[]{:S(2)}) async-start(), calls=%async_computation.15 | async-start | bytes 5640192 | tf_op jit(solution)/shard_map/all_gather | solution.py:165
  211.4 181.2 %all-gather.16.cloned.1.call-start = ((), (), s32[]{:S(2)}) async-start(), calls=%async_computation.14 | async-start | bytes 1769472 | tf_op jit(solution)/shard_map/all_gather | solution.py:39
  228.9 1.5 copy-start.4
  232.6 198.3 %reduce-scatter.15.cloned.1.call-start = ((), (), s32[]{:S(2)}) async-start(), calls=%async_computation.19 | async-start | bytes 1769472 | tf_op jit(solution)/shard_map/reduce_scatter | solution.py:64
  392.6 12.0 %copy-start.33 = (bf16[1152,2304]{1,0:T(8,128)(2,1)S(1)}, bf16[1152,2304]{1,0:T(8,128)(2,1)}, u32[]{:S(2)}) copy-start(bf16[1152,2304]{1,0:T(8,128)(2,1)} %all-gather.18.cloned.1.call-done) | copy-start | bytes 15925252
  403.2 1.4 copy-start.35
  408.8 46.0 %reduce-scatter.13.cloned.1.call-start = ((), (), s32[]{:S(2)}) async-start(), calls=%async_computation.17 | async-start | bytes 1769472 | tf_op jit(solution)/shard_map/reduce_scatter | solution.py:51
  418.0 65.7 %all-gather.24.cloned.1.call-start = ((), (), s32[]{:S(2)}) async-start(), calls=%async_computation.20 | async-start | bytes 1769472 | tf_op jit(solution)/shard_map/all_gather | solution.py:43
  460.7 70.7 %reduce-scatter.17.cloned.1.call-start = ((), (), s32[]{:S(2)}) async-start(), calls=%async_computation.21 | async-start | bytes 1769472 | tf_op jit(solution)/shard_map/reduce_scatter | solution.py:64
  489.1 3.5 copy-start.2
  489.1 3.8 copy-start.11
  502.0 1.2 copy-start.18
  509.4 1.1 copy-start.7
  509.4 22.0 %copy-start.26 = (f32[256]{0:T(256)S(1)}, f32[256]{0:T(256)}, u32[]{:S(2)}) copy-start(f32[256]{0:T(256)} %copy-done.25) | copy-start | bytes 3076
  509.5 156.1 %all-reduce.5.cloned.1.call-start = ((), (), s32[]{:S(2)}) async-start(), calls=%async_computation.25 | async-start | bytes 294912
  510.7 36.2 %copy-start.13 = (bf16[72,8,2,256]{3,1,2,0:T(8,128)(2,1)S(1)}, bf16[72,8,2,256]{3,1,2,0:T(8,128)(2,1)}, u32[]{:S(2)}) copy-start(bf16[72,8,2,256]{3,1,2,0:T(8,128)(2,1)} %copy-done.12) | copy-start | bytes 1769476
  531.5 2.4 copy-start.8
  531.5 15.4 %copy-start.9 = (bf16[512,1152]{1,0:T(8,128)(2,1)S(1)}, bf16[512,1152]{1,0:T(8,128)(2,1)}, u32[]{:S(2)}) copy-start(bf16[512,1152]{1,0:T(8,128)(2,1)} %all-gather.24.cloned.1.call-done) | copy-start | bytes 3538948
  546.8 189.3 %reduce-scatter.25.cloned.1.call-start = ((), (), s32[]{:S(2)}) async-start(), calls=%async_computation.26 | async-start | bytes 3133440
  549.7 1.5 copy-start.19
  549.8 295.5 %reduce-scatter.19.cloned.1.call-start = ((), (), s32[]{:S(2)}) async-start(), calls=%async_computation.22 | async-start | bytes 9400320 | tf_op jit(solution)/shard_map/reduce_scatter | solution.py:272
  558.6 1.3 copy-start.34
  558.6 411.2 %reduce-scatter.21.cloned.1.call-start = ((), (), s32[]{:S(2)}) async-start(), calls=%async_computation.23 | async-start | bytes 11280384 | tf_op jit(solution)/shard_map/reduce_scatter | solution.py:274
  568.5 1.3 copy-start.15
  568.5 526.1 %reduce-scatter.23.cloned.1.call-start = ((), (), s32[]{:S(2)}) async-start(), calls=%async_computation.24 | async-start | bytes 11280384 | tf_op jit(solution)/shard_map/reduce_scatter | solution.py:275
  579.1 3.3 copy-start.28
  579.1 61.6 %copy-start.30 = (f32[256]{0:T(256)S(1)}, f32[256]{0:T(256)}, u32[]{:S(2)}) copy-start(f32[256]{0:T(256)} %get-tuple-element.61) | copy-start | bytes 3076
  579.1 61.6 %copy-start.29 = (f32[256]{0:T(256)S(1)}, f32[256]{0:T(256)}, u32[]{:S(2)}) copy-start(f32[256]{0:T(256)} %get-tuple-element.62) | copy-start | bytes 3076
  579.2 61.6 %copy-start.6 = (f32[256,1152]{1,0:T(8,128)S(1)}, f32[256,1152]{1,0:T(8,128)}, u32[]{:S(2)}) copy-start(f32[256,1152]{1,0:T(8,128)} %copy-done.5) | copy-start | bytes 3538948
  579.2 61.6 %copy-start.27 = (f32[256]{0:T(256)S(1)}, f32[256]{0:T(256)}, u32[]{:S(2)}) copy-start(f32[256]{0:T(256)} %copy-done.25) | copy-start | bytes 3076
  640.8 2.1 copy-start.17
  640.8 24.8 %copy-start.20 = (bf16[1,1152]{1,0:T(2,128)(2,1)S(1)}, bf16[1,1152]{1,0:T(2,128)(2,1)}, u32[]{:S(2)}) copy-start(bf16[1,1152]{1,0:T(2,128)(2,1)} %param.14) | copy-start | bytes 6916
  (6 other events, 4.3 us)
Sparse Core Ops, SparseCore 0:
  91.5 19.0 all-gather.9
  112.9 51.6 all-gather.11
  166.7 37.6 all-gather.13
  208.2 20.6 reduce-scatter.10
  230.8 22.7 all-gather.21
  255.6 56.2 all-gather.19
  314.1 54.9 all-gather.17
  371.2 21.3 all-gather.15
  409.0 21.8 reduce-scatter.14
  432.9 21.8 reduce-scatter.12
  460.9 22.7 all-gather.23
  509.6 21.8 reduce-scatter.16
  546.9 118.5 all-reduce.4
  669.9 66.1 reduce-scatter.24
  740.7 104.5 reduce-scatter.18
  849.8 119.9 reduce-scatter.20
  974.3 120.2 reduce-scatter.22
where the time goes:
time: 1110 us; the launch traced here: 1100 us
  waiting for transfers between devices  796 us (72%)
  blocking collectives  141 us (13%)
  matrix products  90.2 us (8%)
  other arithmetic  28 us (3%)
  local copies, waits for them, and re-layouts  27.5 us (2%)
  between operations  14.9 us (1%)
    reduce_scatter x1, waiting for transfers between devices, per_device(): lax.psum_scatter(fc2_grad, 'dp', scatter_dimension=1, tiled=True)  125 us
    reduce_scatter x1, waiting for transfers between devices, per_device(): lax.psum_scatter(fc1_grad, 'dp', scatter_dimension=0, tiled=True)  124 us
    reduce_scatter x1, waiting for transfers between devices, per_device(): lax.psum_scatter(qkv_grad, 'dp', scatter_dimension=0, tiled=True)  109 us
    unnamed x19, waiting for transfers between devices  93.4 us
    all_gather x1, blocking collectives, per_device(): every_cond = lax.all_gather(silu_cond, ('dp', 'tensor'), axis=0, tiled=True)  70.5 us
    all_gather x1, waiting for transfers between devices, per_device(): lax.all_gather(w_fc2, 'dp', axis=1, tiled=True)  58.4 us
    psum x1, blocking collectives, per_device(): lax.psum((qv_bias_grad, proj_bias_grad, fc1_bias_grad, fc2_bias_grad), 'dp')  58.3 us
    all_gather x1, waiting for transfers between devices, per_device(): lax.all_gather(w_qkv, 'dp', axis=0, tiled=True)  53.9 us
  transfers between devices with their start and end apart: 18, of which 18 were waited for; matrix products, arithmetic and copies ran while one was open for 7% of the time, Pallas kernels for 0%

commit v1 on v0

--- a/solution.py
+++ b/solution.py
@@ -7,6 +7,27 @@
 
 HEAD_DIM = 72
 eps = 1e-06
+
+
+def collect(x, axis, dim):
+    count, index, width = (lax.axis_size(axis), lax.axis_index(axis), x.shape[dim])
+    ahead = [(i, (i + 1) % count) for i in range(count)]
+    left = [(i, (i - 1) % count) for i in range(count)]
+    out = jnp.zeros((*x.shape[:dim], count * width, *x.shape[dim + 1 :]), x.dtype)
+    out = lax.dynamic_update_slice_in_dim(out, x, index * width, axis=dim)
+    from_left = from_right = x
+    middle = count // 2
+    for hop in range(1, middle + 1):
+        from_left = lax.ppermute(from_left, axis, ahead)
+        out = lax.dynamic_update_slice_in_dim(
+            out, from_left, (index - hop) % count * width, axis=dim
+        )
+        if hop < count - middle:
+            from_right = lax.ppermute(from_right, axis, left)
+            out = lax.dynamic_update_slice_in_dim(
+                out, from_right, (index + hop) % count * width, axis=dim
+            )
+    return out
 
 
 def normalize(values):
@@ -160,7 +181,7 @@
     scale_mlp = modul[:, 4]
     gate_mlp = modul[:, 5]
     qkv_full, proj_full, fc1_full, fc2_full = (
-        lax.all_gather(w_qkv, "dp", axis=0, tiled=True),
+        collect(w_qkv, "dp", 0),
         lax.all_gather(w_proj, "dp", axis=1, tiled=True),
         lax.all_gather(w_fc1, "dp", axis=0, tiled=True),
         lax.all_gather(w_fc2, "dp", axis=1, tiled=True),

time: 1110 us -> 1250 us (1.13)
  local copies, waits for them, and re-layouts: 27.5 us -> 178 us
  waiting for transfers between devices: 796 us -> 756 us
  starting transfers between devices: 3.99 us -> 33.6 us
    dynamic_update_slice x0 -> x16, local copies, waits for them, and re-layouts: none -> 136 us  [the longest x8 67.9 us: collect(): lax.dynamic_update_slice_in_dim(out, from_left, (index - hop) % count * w...]
    ppermute x0 -> x15, starting transfers between devices: none -> 29.5 us  [the longest x7 28.8 us: collect(): from_right = lax.ppermute(from_right, axis, left)]
    all_gather x2, waiting for transfers between devices: 41 us -> 15.2 us  [gather_rows(): return lax.all_gather(values, 'tensor', axis=0, tiled=True)]
    all_gather x1, waiting for transfers between devices: 53.9 us -> 31.4 us  [per_device(): lax.all_gather(w_qkv, 'dp', axis=0, tiled=True)]
    all_gather x1, waiting for transfers between devices: 22.1 us -> 0.02 us  [per_device(): lax.all_gather(w_proj, 'dp', axis=1, tiled=True)]
    ppermute x0 -> x15, waiting for transfers between devices: none -> 21.5 us  [the longest x8 15.2 us: collect(): from_left = lax.ppermute(from_left, axis, ahead)]
  transfers between devices with their start and end apart: 18 -> 33, of which waited for: 18 -> 27; matrix products, arithmetic and copies ran while one was open for 7% -> 20% of each run, Pallas kernels for 0% -> 0%
where the time goes in v1:
time: 1250 us; the launch traced here: 1240 us
  waiting for transfers between devices  756 us (60%)
  local copies, waits for them, and re-layouts  178 us (14%)
  blocking collectives  136 us (11%)
  matrix products  92.7 us (7%)
  starting transfers between devices  33.6 us (3%)
  other arithmetic  27.3 us (2%)
  between operations  15.3 us (1%)
    reduce_scatter x1, waiting for transfers between devices, per_device(): lax.psum_scatter(fc2_grad, 'dp', scatter_dimension=1, tiled=True)  125 us
    reduce_scatter x1, waiting for transfers between devices, per_device(): lax.psum_scatter(fc1_grad, 'dp', scatter_dimension=0, tiled=True)  124 us
    reduce_scatter x1, waiting for transfers between devices, per_device(): lax.psum_scatter(qkv_grad, 'dp', scatter_dimension=0, tiled=True)  109 us
    unnamed x19, waiting for transfers between devices  92.3 us
    dynamic_update_slice x8, local copies, waits for them, and re-layouts, collect(): lax.dynamic_update_slice_in_dim(out, from_left, (index - hop) % count * w...  67.9 us
    all_gather x1, blocking collectives, per_device(): every_cond = lax.all_gather(silu_cond, ('dp', 'tensor'), axis=0, tiled=True)  66 us
    dynamic_update_slice x7, local copies, waits for them, and re-layouts, collect(): lax.dynamic_update_slice_in_dim(out, from_right, (index + hop) % count *...  60 us
    all_gather x1, waiting for transfers between devices, per_device(): lax.all_gather(w_fc1, 'dp', axis=0, tiled=True)  58.5 us
  transfers between devices with their start and end apart: 33, of which 27 were waited for; matrix products, arithmetic and copies ran while one was open for 20% of the time, Pallas kernels for 0%

profile of v1, /device:TPU:0, one launch (start us, length us, event | category | flops | bytes accessed | tf_op | source)
XLA Modules:
  0.0 1239.0 jit_solution(4821006069948169036)
XLA Ops:
  7.8 5.0 collective-permute-start.1
  13.5 66.0 %all-gather = bf16[32,1,1152]{2,1,0:T(2,128)(2,1)S(1)} all-gather(bf16[1,1,1152]{2,1,0:T(2,128)(2,1)S(1)} %get-tuple-element.80), channel_id=1, replica_groups=mesh['dp'=16,'tensor'=2] {'dp','tensor'}, dimensions={0}, use_global_device_ids=true | all-gather | bytes 76032 | tf_op jit(solution)/shard_map/all_gather | solution.py:170
  85.4 5.6 all-to-all-done
  95.5 4.7 collective-permute-start.5
  113.0 4.7 collective-permute-start.9
  121.7 4.7 collective-permute-start.11
  130.5 4.8 collective-permute-start.13
  140.9 8.0 dynamic_update_slice.60
  149.1 7.8 dynamic_update_slice.61
  157.2 8.6 dynamic_update_slice.62
  166.1 8.6 dynamic_update_slice.63
  175.0 8.6 dynamic_update_slice.64
  183.9 8.6 dynamic_update_slice.65
  192.7 8.6 dynamic_update_slice.66
  201.6 8.5 dynamic_update_slice.67
  210.4 8.6 dynamic_update_slice.68
  219.3 8.5 dynamic_update_slice.69
  228.1 8.6 dynamic_update_slice.70
  237.0 8.6 dynamic_update_slice.71
  246.8 8.5 dynamic_update_slice.72
  256.6 8.6 dynamic_update_slice.73
  266.4 8.5 dynamic_update_slice.74
  276.2 8.7 dynamic_update_slice.75
  285.0 5.0 fusion.53
  312.1 20.8 %reduce-scatter.11.cloned.1.call-done = bf16[256,1152]{1,0:T(8,128)(2,1)} async-done(((bf16[512,1152]{1,0:T(8,128)(2,1)}), bf16[256,1152]{1,0:T(8,128)(2,1)}) %reduce-scatter.11.cloned.1.call-update) | async-done | bytes 589840 | tf_op jit(solution)/shard_map/reduce_scatter | solution.py:72
  337.1 20.5 %all-gather.20.cloned.1.call-done = bf16[512,1152]{1,0:T(8,128)(2,1)} async-done(((bf16[256,1152]{1,0:T(8,128)(2,1)}), bf16[512,1152]{1,0:T(8,128)(2,1)}) %all-gather.20.cloned.1.call-update) | async-done | bytes 1179664 | tf_op jit(solution)/shard_map/all_gather | solution.py:64
  357.6 58.4 %all-gather.18.cloned.1.call-done = bf16[2304,1152]{0,1:T(8,128)(2,1)} async-done(((bf16[2304,72]{0,1:T(8,128)(2,1)}), bf16[2304,1152]{0,1:T(8,128)(2,1)}) %all-gather.18.cloned.1.call-update) | async-done | bytes 5308432 | tf_op jit(solution)/shard_map/all_gather | solution.py:187
  416.0 8.2 fusion.89
  424.2 15.2 %all-gather.14.cloned.1.call-done = bf16[512,1152]{1,0:T(8,128)(2,1)} async-done(((bf16[256,1152]{1,0:T(8,128)(2,1)}), bf16[512,1152]{1,0:T(8,128)(2,1)}) %all-gather.14.cloned.1.call-update) | async-done | bytes 1179664 | tf_op jit(solution)/shard_map/all_gather | solution.py:60
  439.4 58.5 %all-gather.16.cloned.1.call-done = bf16[1152,2304]{1,0:T(8,128)(2,1)} async-done(((bf16[72,2304]{1,0:T(8,128)(2,1)}), bf16[1152,2304]{1,0:T(8,128)(2,1)}) %all-gather.16.cloned.1.call-update) | async-done | bytes 5308432 | tf_op jit(solution)/shard_map/all_gather | solution.py:186
  497.9 10.4 convert_reduce_fusion
  514.1 9.0 convolution_convert_fusion.1
  523.2 11.4 reduce-scatter.15.cloned.1.call-done
  537.6 21.0 %reduce-scatter.13.cloned.1.call-done = bf16[256,1152]{1,0:T(8,128)(2,1)} async-done(((bf16[512,1152]{1,0:T(8,128)(2,1)}), bf16[256,1152]{1,0:T(8,128)(2,1)}) %reduce-scatter.13.cloned.1.call-update) | async-done | bytes 589840 | tf_op jit(solution)/shard_map/reduce_scatter | solution.py:72
  565.3 22.1 %all-gather.22.cloned.1.call-done = bf16[512,1152]{1,0:T(8,128)(2,1)} async-done(((bf16[256,1152]{1,0:T(8,128)(2,1)}), bf16[512,1152]{1,0:T(8,128)(2,1)}) %all-gather.22.cloned.1.call-update) | async-done | bytes 1179664 | tf_op jit(solution)/shard_map/all_gather | solution.py:64
  610.1 31.4 %all-gather.24.cloned.1.call-done = bf16[1152,3,576]{2,0,1:T(8,128)(2,1)} async-done(((bf16[72,3,576]{2,0,1:T(8,128)(2,1)}), bf16[1152,3,576]{2,0,1:T(8,128)(2,1)}) %all-gather.24.cloned.1.call-update) | async-done | bytes 3981328 | tf_op jit(solution)/shard_map/all_gather | solution.py:222
  641.4 6.8 fusion.8
  649.5 19.3 %reduce-scatter.17.cloned.1.call-done = bf16[256,1152]{1,0:T(8,128)(2,1)} async-done(((bf16[512,1152]{1,0:T(8,128)(2,1)}), bf16[256,1152]{1,0:T(8,128)(2,1)}) %reduce-scatter.17.cloned.1.call-update) | async-done | bytes 589840 | tf_op jit(solution)/shard_map/reduce_scatter | solution.py:85
  671.8 11.8 all_to_all.26
  688.6 7.6 fusion.51
  697.5 8.7 fusion.91
  707.5 9.3 fusion.86
  720.1 58.3 %all-reduce.2 = (f32[2,576]{1,0:T(2,128)}, f32[1152]{0:T(1024)}, f32[2304]{0:T(1024)}, f32[1152]{0:T(1024)}) all-reduce(f32[2,576]{1,0:T(2,128)S(1)} %pad_maximum_fusion, f32[1152]{0:T(1024)S(1)} %convert_reduce_fusion.2, f32[2304]{0:T(1024)S(1)} %copy-done.45, ...), channel_id=1, replica_groups=mesh['dp'=16,'tensor'=2] {'dp'}, use_global_device_ids=true, to_apply=%region_25.26 | all-reduce | flops 5760 | bytes 46080 | tf_op jit(solution)/shard_map/psum | solution.py:298
  781.9 21.4 %all-reduce.5.cloned.1.call-done = f32[32,1152]{1,0:T(8,128)} async-done(((f32[32,1152]{1,0:T(8,128)}), f32[32,1152]{1,0:T(8,128)}) %all-reduce.5.cloned.1.call-update) | async-done | bytes 147472
  804.6 69.2 %reduce-scatter.25.cloned.1.call-done = f32[576,72]{0,1:T(8,128)} async-done(((f32[576,1152]{0,1:T(8,128)}), f32[576,72]{0,1:T(8,128)}) %reduce-scatter.25.cloned.1.call-update) | async-done | bytes 165904
  873.8 109.2 %reduce-scatter.19.cloned.1.call-done = f32[72,3,576]{2,0,1:T(8,128)} async-done(((f32[1152,3,576]{2,0,1:T(8,128)}), f32[72,3,576]{2,0,1:T(8,128)}) %reduce-scatter.19.cloned.1.call-update) | async-done | bytes 497680 | tf_op jit(solution)/shard_map/reduce_scatter | solution.py:293
  983.0 124.5 %reduce-scatter.21.cloned.1.call-done = f32[72,2304]{1,0:T(8,128)} async-done(((f32[1152,2304]{1,0:T(8,128)}), f32[72,2304]{1,0:T(8,128)}) %reduce-scatter.21.cloned.1.call-update) | async-done | bytes 663568 | tf_op jit(solution)/shard_map/reduce_scatter | solution.py:295
  1107.5 124.8 %reduce-scatter.23.cloned.1.call-done = f32[2304,72]{0,1:T(8,128)} async-done(((f32[2304,1152]{0,1:T(8,128)}), f32[2304,72]{0,1:T(8,128)}) %reduce-scatter.23.cloned.1.call-update) | async-done | bytes 663568 | tf_op jit(solution)/shard_map/reduce_scatter | solution.py:296
  (269 shorter events, 129.6 us)
Async XLA Ops:
  7.2 73.0 %copy-start = (bf16[1152,216]{0,1:T(8,128)(2,1)S(1)}, bf16[1152,216]{0,1:T(8,128)(2,1)}, u32[]{:S(2)}) copy-start(bf16[1152,216]{0,1:T(8,128)(2,1)} %param.23) | copy-start | bytes 1492996
  7.2 77.8 %copy-start.3 = (bf16[256,1152]{1,0:T(8,128)(2,1)S(1)}, bf16[256,1152]{1,0:T(8,128)(2,1)}, u32[]{:S(2)}) copy-start(bf16[256,1152]{1,0:T(8,128)(2,1)} %param.13) | copy-start | bytes 1769476
  7.2 78.0 %collective-permute-start = (bf16[72,3,576]{2,0,1:T(8,128)(2,1)}, bf16[72,3,576]{2,0,1:T(8,128)(2,1)S(1)}, u32[]{:S(2)}, u32[]{:S(2)}) collective-permute-start(bf16[72,3,576]{2,0,1:T(8,128)(2,1)} %param.15), channel_id=1, source_target_pairs={{0,2},{2,4},{4,6},{6,8},{8,10},{10,12},{12,14},{14,16},{16,18},{18... | collective-permute-start | bytes 746504 | tf_op jit(solution)/shard_map/ppermute | solution.py:21
  7.8 83.5 %collective-permute-start.1 = (bf16[72,3,576]{2,0,1:T(8,128)(2,1)}, bf16[72,3,576]{2,0,1:T(8,128)(2,1)S(1)}, u32[]{:S(2)}, u32[]{:S(2)}) collective-permute-start(bf16[72,3,576]{2,0,1:T(8,128)(2,1)} %param.15), channel_id=1, source_target_pairs={{0,30},{2,0},{4,2},{6,4},{8,6},{10,8},{12,10},{14,12},{16,14},{18,... | collective-permute-start | bytes 746504 | tf_op jit(solution)/shard_map/ppermute | solution.py:26
  81.1 9.9 all-to-all-start
  83.7 201.3 %all-gather.10.cloned.1.call-start = ((), (), s32[]{:S(2)}) async-start(), calls=%async_computation.10 | async-start | bytes 1769472 | tf_op jit(solution)/shard_map/all_gather | solution.py:60
  84.9 53.0 %copy-start.23 = (bf16[72,3,576]{2,0,1:T(8,128)(2,1)S(1)}, bf16[72,3,576]{2,0,1:T(8,128)(2,1)}, u32[]{:S(2)}) copy-start(bf16[72,3,576]{2,0,1:T(8,128)(2,1)} %param.15) | copy-start | bytes 746500
  85.3 8.7 collective-permute-start.2
  85.4 52.8 %copy-start.43 = (f32[256]{0:T(256)}, f32[256]{0:T(256)S(1)}, u32[]{:S(2)}) copy-start(f32[256]{0:T(256)S(1)} %add_rsqrt_fusion.1) | copy-start | bytes 3076
  91.3 4.2 collective-permute-start.3
  94.0 8.7 collective-permute-start.4
  94.0 44.5 %copy-start.49 = (bf16[2,576]{1,0:T(2,128)(2,1)S(1)}, bf16[2,576]{1,0:T(2,128)(2,1)}, u32[]{:S(2)}) copy-start(bf16[2,576]{1,0:T(2,128)(2,1)} %param.16) | copy-start | bytes 6916
  95.1 210.5 %all-gather.12.cloned.1.call-start = ((), (), s32[]{:S(2)}) async-start(), calls=%async_computation.11 | async-start | bytes 1566720 | tf_op jit(solution)/shard_map/all_gather | solution.py:185
  95.5 8.7 collective-permute-start.5
  102.7 8.7 collective-permute-start.6
  104.2 8.7 collective-permute-start.7
  111.5 8.7 collective-permute-start.8
  113.0 8.7 collective-permute-start.9
  120.2 8.7 collective-permute-start.10
  121.7 8.7 collective-permute-start.11
  129.0 8.9 collective-permute-start.12
  130.5 134.7 %collective-permute-start.13 = (bf16[72,3,576]{2,0,1:T(8,128)(2,1)}, bf16[72,3,576]{2,0,1:T(8,128)(2,1)}, u32[]{:S(2)}, u32[]{:S(2)}) collective-permute-start(bf16[72,3,576]{2,0,1:T(8,128)(2,1)} %collective-permute-done.11), channel_id=1, source_target_pairs={{0,30},{2,0},{4,2},{6,4},{8,6},{10,8},{12,10},{14,12},{16,14},{18,... | collective-permute-start | bytes 746504 | tf_op jit(solution)/shard_map/ppermute | solution.py:26
  137.8 137.2 %collective-permute-start.14 = (bf16[72,3,576]{2,0,1:T(8,128)(2,1)}, bf16[72,3,576]{2,0,1:T(8,128)(2,1)}, u32[]{:S(2)}, u32[]{:S(2)}) collective-permute-start(bf16[72,3,576]{2,0,1:T(8,128)(2,1)} %collective-permute-done.12), channel_id=1, source_target_pairs={{0,2},{2,4},{4,6},{6,8},{8,10},{10,12},{12,14},{14,16},{16,18},{18... | collective-permute-start | bytes 746504 | tf_op jit(solution)/shard_map/ppermute | solution.py:21
  137.8 195.0 %reduce-scatter.11.cloned.1.call-start = ((), (), s32[]{:S(2)}) async-start(), calls=%async_computation.12 | async-start | bytes 1769472 | tf_op jit(solution)/shard_map/reduce_scatter | solution.py:72
  183.6 17.7 %copy-start.29 = (bf16[72,3,576]{2,0,1:T(8,128)(2,1)S(1)}, bf16[72,3,576]{2,0,1:T(8,128)(2,1)}, u32[]{:S(2)}) copy-start(bf16[72,3,576]{2,0,1:T(8,128)(2,1)} %copy-done.28) | copy-start | bytes 746500
  309.5 48.2 %all-gather.20.cloned.1.call-start = ((), (), s32[]{:S(2)}) async-start(), calls=%async_computation.17 | async-start | bytes 1769472 | tf_op jit(solution)/shard_map/all_gather | solution.py:64
  311.4 104.6 %all-gather.18.cloned.1.call-start = ((), (), s32[]{:S(2)}) async-start(), calls=%async_computation.15 | async-start | bytes 5640192 | tf_op jit(solution)/shard_map/all_gather | solution.py:187
  312.0 127.3 %all-gather.14.cloned.1.call-start = ((), (), s32[]{:S(2)}) async-start(), calls=%async_computation.13 | async-start | bytes 1769472 | tf_op jit(solution)/shard_map/all_gather | solution.py:60
  334.8 89.4 %copy-start.40 = (f32[256]{0:T(256)}, f32[256]{0:T(256)S(1)}, u32[]{:S(2)}) copy-start(f32[256]{0:T(256)S(1)} %add_rsqrt_fusion) | copy-start | bytes 3076
  336.1 161.8 %all-gather.16.cloned.1.call-start = ((), (), s32[]{:S(2)}) async-start(), calls=%async_computation.14 | async-start | bytes 5640192 | tf_op jit(solution)/shard_map/all_gather | solution.py:186
  336.8 197.8 %reduce-scatter.15.cloned.1.call-start = ((), (), s32[]{:S(2)}) async-start(), calls=%async_computation.18 | async-start | bytes 1769472 | tf_op jit(solution)/shard_map/reduce_scatter | solution.py:85
  514.0 44.7 %reduce-scatter.13.cloned.1.call-start = ((), (), s32[]{:S(2)}) async-start(), calls=%async_computation.16 | async-start | bytes 1769472 | tf_op jit(solution)/shard_map/reduce_scatter | solution.py:72
  523.1 64.3 %all-gather.22.cloned.1.call-start = ((), (), s32[]{:S(2)}) async-start(), calls=%async_computation.19 | async-start | bytes 1769472 | tf_op jit(solution)/shard_map/all_gather | solution.py:64
  534.6 24.1 %copy-start.12 = (bf16[256,1152]{1,0:T(8,128)(2,1)S(1)}, bf16[256,1152]{1,0:T(8,128)(2,1)}, u32[]{:S(2)}) copy-start(bf16[256,1152]{1,0:T(8,128)(2,1)} %reduce-scatter.15.cloned.1.call-done) | copy-start | bytes 1769476
  564.5 77.0 %all-gather.24.cloned.1.call-start = ((), (), s32[]{:S(2)}) async-start(), calls=%async_computation.20 | async-start | bytes 4700160 | tf_op jit(solution)/shard_map/all_gather | solution.py:222
  565.2 103.5 %reduce-scatter.17.cloned.1.call-start = ((), (), s32[]{:S(2)}) async-start(), calls=%async_computation.21 | async-start | bytes 1769472 | tf_op jit(solution)/shard_map/reduce_scatter | solution.py:85
  610.1 38.4 %copy-start.42 = (bf16[1152]{0:T(1024)(128)(2,1)S(1)}, bf16[1152]{0:T(1024)(128)(2,1)}, u32[]{:S(2)}) copy-start(bf16[1152]{0:T(1024)(128)(2,1)} %get-tuple-element.78) | copy-start | bytes 6916
  648.2 21.7 %copy-start.44 = (f32[256]{0:T(256)S(1)}, f32[256]{0:T(256)}, u32[]{:S(2)}) copy-start(f32[256]{0:T(256)} %copy-done.43) | copy-start | bytes 3076
  648.2 155.0 %all-reduce.5.cloned.1.call-start = ((), (), s32[]{:S(2)}) async-start(), calls=%async_computation.25 | async-start | bytes 294912
  649.4 35.1 %copy-start.15 = (bf16[512,1152]{1,0:T(8,128)(2,1)S(1)}, bf16[512,1152]{1,0:T(8,128)(2,1)}, u32[]{:S(2)}) copy-start(bf16[512,1152]{1,0:T(8,128)(2,1)} %all-gather.22.cloned.1.call-done) | copy-start | bytes 3538948
  649.4 35.1 %copy-start.19 = (bf16[72,8,2,256]{3,1,2,0:T(8,128)(2,1)S(1)}, bf16[72,8,2,256]{3,1,2,0:T(8,128)(2,1)}, u32[]{:S(2)}) copy-start(bf16[72,8,2,256]{3,1,2,0:T(8,128)(2,1)} %copy-done.18) | copy-start | bytes 1769476
  684.4 189.4 %reduce-scatter.25.cloned.1.call-start = ((), (), s32[]{:S(2)}) async-start(), calls=%async_computation.26 | async-start | bytes 3133440
  687.4 295.6 %reduce-scatter.19.cloned.1.call-start = ((), (), s32[]{:S(2)}) async-start(), calls=%async_computation.22 | async-start | bytes 9400320 | tf_op jit(solution)/shard_map/reduce_scatter | solution.py:293
  696.2 411.2 %reduce-scatter.21.cloned.1.call-start = ((), (), s32[]{:S(2)}) async-start(), calls=%async_computation.23 | async-start | bytes 11280384 | tf_op jit(solution)/shard_map/reduce_scatter | solution.py:295
  706.2 526.1 %reduce-scatter.23.cloned.1.call-start = ((), (), s32[]{:S(2)}) async-start(), calls=%async_computation.24 | async-start | bytes 11280384 | tf_op jit(solution)/shard_map/reduce_scatter | solution.py:296
  716.8 61.6 %copy-start.7 = (f32[256,1152]{1,0:T(8,128)S(1)}, f32[256,1152]{1,0:T(8,128)}, u32[]{:S(2)}) copy-start(f32[256,1152]{1,0:T(8,128)} %copy-done.6) | copy-start | bytes 3538948
  716.8 61.6 %copy-start.14 = (bf16[256,1152]{1,0:T(8,128)(2,1)S(1)}, bf16[256,1152]{1,0:T(8,128)(2,1)}, u32[]{:S(2)}) copy-start(bf16[256,1152]{1,0:T(8,128)(2,1)} %reduce-scatter.17.cloned.1.call-done) | copy-start | bytes 1769476
  778.5 24.8 %copy-start.38 = (bf16[1,1152]{1,0:T(2,128)(2,1)S(1)}, bf16[1,1152]{1,0:T(2,128)(2,1)}, u32[]{:S(2)}) copy-start(bf16[1,1152]{1,0:T(2,128)(2,1)} %param.14) | copy-start | bytes 6916
  (39 other events, 192.9 us)
Sparse Core Ops, SparseCore 0:
  95.2 24.1 all-gather.9
  138.0 40.5 all-gather.11
  309.6 23.2 reduce-scatter.10
  334.9 22.7 all-gather.19
  359.7 56.2 all-gather.17
  418.0 21.3 all-gather.13
  441.5 56.2 all-gather.15
  514.1 20.4 reduce-scatter.14
  536.8 21.8 reduce-scatter.12
  564.6 22.7 all-gather.21
  589.6 51.7 all-gather.23
  648.4 20.3 reduce-scatter.16
  684.6 118.6 all-reduce.4
  807.6 66.1 reduce-scatter.24
  878.4 104.5 reduce-scatter.18
  987.5 119.9 reduce-scatter.20
  1112.0 120.2 reduce-scatter.22
